TPU v7x, 8 devices: a whole 2x2x1 slice. The times are simulated.
8 devices in a mesh: data: 2 (over z, y), model: 4 (over x, core).
Axes of the slice: x: 2, y: 2, z: 1, core: 2. Of those that a mesh axis runs over, the one named last changes fastest.
Arguments:
- x_in: bfloat16 [128, 6144], P(('data', 'model')), parts along dimension 0
- dy_in: bfloat16 [128, 6144], P(('data', 'model')), parts along dimension 0
- w_query: bfloat16 [6144, 48, 128], P(None, 'model')
- w_key: bfloat16 [6144, 128], replicated
- w_value: bfloat16 [6144, 128], replicated
- w_out: bfloat16 [48, 128, 6144], P('model')
Outputs:
- output 1: bfloat16 [128, 6144], P(('data', 'model')), parts along dimension 0
- output 2: float32 [12288, 48, 128], P('data', 'model'), parts along dimension 0
- output 3: float32 [12288, 128], P(('data', 'model')), parts along dimension 0
- output 4: float32 [12288, 128], P(('data', 'model')), parts along dimension 0
- output 5: float32 [96, 128, 6144], P(('data', 'model')), parts along dimension 0
There are 2 independent parts. A program takes and returns all parts, laid end to end along the dimension named above; an argument that names none is the same for every part.
All inputs are finite; a program needn't handle non-finite values.
Results may differ from a plain program's by a relative error of at most 0.0107.
Values are sent between devices in bfloat16 or wider.
A program may use at most 1 GiB of HBM per device.

v0:
```python
import functools
import math
import jax
import jax.numpy as jnp
from jax import lax
from jax.experimental import pallas as pl
from jax.experimental.pallas import tpu as pltpu
from jax.sharding import PartitionSpec as P

MESH = pl.DeviceIdType.MESH
ANY = pl.BlockSpec(memory_space=pl.ANY)
VM = pl.BlockSpec(memory_space=pltpu.VMEM)
F32 = jnp.float32
BF = jnp.bfloat16
NT = (((1,), (1,)), ((), ()))
TN = (((0,), (0,)), ((), ()))

T, D, HL, E, R = 64, 6144, 12, 128, 16
NP = HL // 2
NC = 4
LEAD = 1
DC = D // NC
NX = 8
XC = D // NX
N1 = 512
N2 = 256


def attend_kernel(x_ref, dy_ref, wq_ref, wk_ref, wv_ref, wo_ref,
                  xt_ref, dyg_ref, ot_ref, dq_ref, dkv_ref, wkv, dxk_ref, dxs_ref,
                  xg, wq, wo, qacc, kvacc, doacc, dot_acc, q_s, o_s, do_s, dqp, part, keep, send, got,
                  lsem, wsem, link_s, link_r, pair_s, pair_r, fwd_s, fwd_r, ex_s, ex_r, red_s, red_r):
    scale = 1.0 / math.sqrt(E)
    m = lax.axis_index("model")
    core, chip = m % 2, m // 2
    partner = chip * 2 + (1 - core)
    counter = (1 - chip) * 2 + core
    diag = (1 - chip) * 2 + (1 - core)
    own = pl.ds(pl.multiple_of(m * R, R), R)
    far = pl.ds(pl.multiple_of(counter * R, R), R)
    bufs = (dyg_ref, xg)

    def cols(c):
        return pl.ds(c * DC, DC)

    loads = [pltpu.make_async_copy(s, g.at[own], lsem.at[a]) for a, (s, g) in enumerate(((dy_ref, dyg_ref), (x_ref, xg)))]
    for cp in loads:
        cp.start()
    wkv_cp = [pltpu.make_async_copy(s, wkv.at[:, pl.ds(j * E, E)], wsem.at[j]) for j, s in enumerate((wk_ref, wv_ref))]
    wq_cp = [[pltpu.make_async_copy(wq_ref.at[:, j, cols(c), :], wq.at[:, cols(c), pl.ds(j * E, E)], wsem.at[2 + 2 * c + j])
              for j in range(2)] for c in range(NC)]
    wo_cp = [pltpu.make_async_copy(wo_ref.at[:, cols(c)], wo.at[:, cols(c)], wsem.at[2 + 2 * NC + c]) for c in range(NC)]
    for cp in wo_cp[:NC // 2]:
        cp.start(priority=1)

    barrier = pltpu.get_barrier_semaphore()
    for peer in (partner, counter, diag):
        pl.semaphore_signal(barrier, inc=1, device_id={"model": peer}, device_id_type=MESH)
    pl.semaphore_wait(barrier, 3)

    link, pair, fwd = [], [], []
    for a in range(2):
        g = bufs[a]
        loads[a].wait()
        link.append([pltpu.make_async_remote_copy(g.at[own, cols(c)], g.at[own, cols(c)], link_s.at[a, c], link_r.at[a, c],
                                                  device_id={"model": counter}, device_id_type=MESH) for c in range(NC)])
        pair.append(pltpu.make_async_remote_copy(g.at[own], g.at[own], pair_s.at[a], pair_r.at[a],
                                                 device_id={"model": partner}, device_id_type=MESH))
        fwd.append([pltpu.make_async_remote_copy(g.at[far, cols(c)], g.at[far, cols(c)], fwd_s.at[a, c], fwd_r.at[a, c],
                                                 device_id={"model": partner}, device_id_type=MESH) for c in range(NC)])
        for cp in link[a]:
            cp.start()
        pair[a].start()

    for cp in wo_cp[NC // 2:] + wkv_cp:
        cp.start(priority=1)

    def relay(i):
        a, c = divmod(i, NC)
        if a < 2:
            link[a][c].wait_recv()
            fwd[a][c].start()

    for i in range(LEAD):
        relay(i)
    pair[0].wait_recv()
    for c in range(NC):
        relay(c + LEAD)
        fwd[0][c].wait_recv()
        wo_cp[c].wait()
        for cp in wq_cp[c]:
            cp.start(priority=1)
        dyc = dyg_ref[:, cols(c)]
        dyct = dyc.T
        for p in range(2):
            base = p * (N1 + N2)
            by_rows, by_cols = None, None
            for k in range(DC // 256):
                ks = pl.ds(c * DC + k * 256, 256)
                t1 = lax.dot_general(dyc[:, k * 256:(k + 1) * 256], wo[pl.ds(base, N1), ks], NT, preferred_element_type=F32)
                t2 = jnp.dot(wo[pl.ds(base + N1, N2), ks], dyct[k * 256:(k + 1) * 256, :], preferred_element_type=F32)
                by_rows = t1 if by_rows is None else by_rows + t1
                by_cols = t2 if by_cols is None else by_cols + t2
            if c == 0:
                doacc[p] = by_rows
                dot_acc[p] = by_cols
            else:
                doacc[p] += by_rows
                dot_acc[p] += by_cols
    for p in range(2):
        for j in range(6):
            rows = pl.ds((p * 6 + j) * T, T)
            if j < 4:
                do_s[rows, :] = doacc[p, :, j * E:(j + 1) * E].astype(BF)
            else:
                do_s[rows, :] = dot_acc[p, (j - 4) * E:(j - 3) * E, :].T.astype(BF)
    pair[1].wait_recv()
    for cp in wkv_cp:
        cp.wait()
    for c in range(NC):
        relay(NC + c + LEAD)
        fwd[1][c].wait_recv()
        for cp in wq_cp[c]:
            cp.wait()
        xc = xg[:, cols(c)]
        for p in range(NP):
            part_q = jnp.dot(xc, wq[p, cols(c), :], preferred_element_type=F32)
            if c == 0:
                qacc[p] = part_q
            else:
                qacc[p] += part_q
        part_kv = jnp.dot(xc, wkv[cols(c), :], preferred_element_type=F32)
        if c == 0:
            kvacc[...] = part_kv
        else:
            kvacc[...] += part_kv
        xt_ref[cols(c), :] = xc.T
    kv = kvacc[...].astype(BF)
    keys, vals = kv[:, :E], kv[:, E:]
    for p in range(NP):
        qp = qacc[p].astype(BF)
        q_s[pl.ds(2 * p * T, T), :] = qp[:, :E]
        q_s[pl.ds((2 * p + 1) * T, T), :] = qp[:, E:]
    d_attn = do_s[...]
    s = lax.dot_general(q_s[...], keys, NT, preferred_element_type=F32) * scale
    d_probs = lax.dot_general(d_attn, vals, NT, preferred_element_type=F32)
    row = lax.broadcasted_iota(jnp.int32, (HL * T, T), 0) % T
    col = lax.broadcasted_iota(jnp.int32, (HL * T, T), 1)
    s = jnp.where(row >= col, s, -jnp.inf)
    e = jnp.exp(s - jnp.max(s, axis=-1, keepdims=True))
    p32 = e / jnp.sum(e, axis=-1, keepdims=True)
    pb = p32.astype(BF)
    ob = jnp.dot(pb, vals, preferred_element_type=F32).astype(BF)
    o_s[...] = ob
    row_dot = jnp.sum(d_attn.astype(F32) * ob.astype(F32), axis=-1, keepdims=True)
    g = (p32 * (d_probs - row_dot) * scale).astype(BF)
    part[0, :, E:] = lax.dot_general(pb, d_attn, TN, preferred_element_type=F32)
    part[0, :, :E] = lax.dot_general(g, q_s[...], TN, preferred_element_type=F32)
    d_query = jnp.dot(g, keys, preferred_element_type=F32).astype(BF)
    for h in range(HL):
        dqh = d_query[h * T:(h + 1) * T, :]
        dq_ref[:, pl.ds(h * E, E)] = dqh
        for r in range(4):
            slot = (r // 2 + chip) % 2 * 2 + (r % 2 + core) % 2
            dqp[slot, :, pl.ds(h * E, E)] = dqh[r * R:(r + 1) * R, :]
    ex = [pltpu.make_async_remote_copy(part.at[2 * i], part.at[2 * i + 1], ex_s.at[i], ex_r.at[i], device_id={"model": peer}, device_id_type=MESH)
          for i, peer in enumerate((partner, counter))]
    ex[0].start()
    lhs = dqp[...].reshape(T, HL * E)
    red = [pltpu.make_async_remote_copy(send.at[:, :, pl.ds(c * XC, XC)], got.at[:, :, pl.ds(c * XC, XC)], red_s.at[c], red_r.at[c],
                                        device_id={"model": partner}, device_id_type=MESH) for c in range(NX)]

    lhst = lhs.T

    def dx_chunk(c):
        base = c * XC
        by_rows, by_cols = None, None
        for p in range(NP):
            ps = slice(p * 2 * E, (p + 1) * 2 * E)
            t1 = lax.dot_general(lhs[:, ps], wq[p, pl.ds(base, N1), :], NT, preferred_element_type=F32)
            t2 = jnp.dot(wq[p, pl.ds(base + N1, N2), :], lhst[ps, :], preferred_element_type=F32)
            by_rows = t1 if by_rows is None else by_rows + t1
            by_cols = t2 if by_cols is None else by_cols + t2
        by_cols = by_cols.T
        for k in range(4):
            dst, r = (send if k % 2 else keep), slice(k * R, (k + 1) * R)
            dst[k // 2, :, pl.ds(base, N1)] = by_rows[r, :]
            dst[k // 2, :, pl.ds(base + N1, N2)] = by_cols[r, :]

    def dx_sum(c):
        rows = pl.ds(c * XC, XC)
        red[c].wait_recv()
        dxk_ref[:, rows] = keep[0, :, rows] + got[0, :, rows]
        dxs_ref[:, rows] = keep[1, :, rows] + got[1, :, rows]

    for c in range(NX):
        dx_chunk(c)
        if c == 0:
            for h in range(HL):
                ot_ref[pl.ds(h * E, E), :] = o_s[pl.ds(h * T, T), :].T
        if c == 1:
            ex[0].wait_recv()
            part[2] = part[0] + part[1]
        if c == 2:
            ex[1].start()
        if c >= 1:
            red[c - 1].start()
    for c in range(NX - 2):
        dx_sum(c)
    red[NX - 1].start()
    dx_sum(NX - 2)
    ex[1].wait_recv()
    dkv_ref[...] = (part[2] + part[3]).astype(BF)
    dx_sum(NX - 1)
    for a in range(2):
        pair[a].wait_send()
        for c in range(NC):
            link[a][c].wait_send()
            fwd[a][c].wait_send()
    for cp in ex + red:
        cp.wait_send()


NB = 4
CW = D // 2
RQ = D // 4


def grads_kernel(xt_ref, dyg_ref, ot_ref, dq_ref, dkv_ref, wkv_ref, dx_ref, dwq_ref, dwo_ref, dwk_ref, dwv_ref, dxo_ref,
                 bo, bq, bkv, osem, qsem, ksem):
    m = lax.axis_index("model")

    def o_copy(i, j, slot):
        return pltpu.make_async_copy(bo.at[slot], dwo_ref.at[pl.ds(pl.multiple_of(i * E, E), E), pl.ds(j * CW, CW)], osem.at[slot])

    def q_copy(i, j, slot):
        rows = pl.ds(pl.multiple_of((i % 2) * (2 * RQ) + j * RQ, RQ), RQ)
        return pltpu.make_async_copy(bq.at[slot], dwq_ref.at[i // 2, :, rows, :], qsem.at[slot])

    def body(i, carry):
        ot = ot_ref[pl.ds(pl.multiple_of(i * E, E), E), :]
        dq = dq_ref[:, pl.ds(pl.multiple_of((i // 2) * 2 * E, 2 * E), 2 * E)]
        for j in range(2):
            slot = (i % 2) * 2 + j

            @pl.when(i >= 2)
            def _():
                o_copy(i - 2, j, slot).wait()

            bo[slot] = jnp.dot(ot, dyg_ref[:, j * CW:(j + 1) * CW], preferred_element_type=F32)
            o_copy(i, j, slot).start()

            @pl.when(i >= 2)
            def _():
                q_copy(i - 2, j, slot).wait()

            rows = pl.ds(pl.multiple_of((i % 2) * (2 * RQ) + j * RQ, RQ), RQ)
            v = jnp.dot(xt_ref[rows, :], dq, preferred_element_type=F32)
            bq[slot, 0] = v[:, :E]
            bq[slot, 1] = v[:, E:]
            q_copy(i, j, slot).start()
        return carry

    lax.fori_loop(0, HL, body, 0)
    v = jnp.dot(xt_ref[pl.ds(pl.multiple_of(m * RQ, RQ), RQ), :], dkv_ref[...], preferred_element_type=F32)
    bkv[0] = v[:, :E]
    bkv[1] = v[:, E:]
    k_cp = [pltpu.make_async_copy(bkv.at[j], r, ksem.at[j]) for j, r in enumerate((dwk_ref, dwv_ref))]
    for cp in k_cp:
        cp.start()
    mine = dkv_ref[pl.ds(pl.multiple_of(m * R, R), R), :]
    dxo_ref[...] = dx_ref[...] + lax.dot_general(mine, wkv_ref[...], NT, preferred_element_type=F32)
    for i in (HL - 2, HL - 1):
        for j in range(2):
            o_copy(i, j, (i % 2) * 2 + j).wait()
            q_copy(i, j, (i % 2) * 2 + j).wait()
    for cp in k_cp:
        cp.wait()


def solution(mesh):
    tok = P(("data", "model"), None)

    def step(x, dy, w_query, w_key, w_value, w_out):
        wq = jnp.transpose(w_query, (1, 0, 2)).reshape(NP, 2, D, E)
        wo = w_out.reshape(HL * E, D)
        S = jax.ShapeDtypeStruct
        DMA = pltpu.SemaphoreType.DMA
        V = pltpu.VMEM
        xt, dyg, ot, dq, dkv, wkv, dxk, dxs = pl.pallas_call(
            attend_kernel,
            out_shape=[V((D, T), BF), V((T, D), BF), V((HL * E, T), BF), V((T, HL * E), BF), V((T, 2 * E), BF), V((D, 2 * E), BF), V((R, D), F32), S((R, D), F32)],
            in_specs=[ANY] * 6,
            out_specs=[VM] * 8,
            scratch_shapes=[
                V((T, D), BF), V((NP, D, 2 * E), BF), V((HL * E, D), BF), V((NP, T, 2 * E), F32), V((T, 2 * E), F32),
                V((2, T, N1), F32), V((2, N2, T), F32), V((HL * T, E), BF), V((HL * T, E), BF), V((HL * T, E), BF),
                V((4, R, HL * E), BF), V((4, T, 2 * E), F32), V((2, R, D), F32), V((2, R, D), F32), V((2, R, D), F32),
                DMA((2,)), DMA((2 + 3 * NC,)), DMA((2, NC)), DMA((2, NC)), DMA((2,)), DMA((2,)), DMA((2, NC)), DMA((2, NC)),
                DMA((2,)), DMA((2,)), DMA((NX,)), DMA((NX,)),
            ],
            compiler_params=pltpu.CompilerParams(collective_id=0, has_side_effects=True, vmem_limit_bytes=50 * 2**20),
            cost_estimate=pl.CostEstimate(flops=10**10, bytes_accessed=4 * 10**7, transcendentals=0),
            name="attend",
        )(x, dy, wq, w_key, w_value, wo)
        far = lax.ppermute(dxs, "model", [(0, 2), (2, 0), (1, 3), (3, 1)])
        dwq, dwo, dwk, dwv, dxo = pl.pallas_call(
            grads_kernel,
            out_shape=[S((NP, 2, D, E), F32), S((HL * E, D), F32), S((RQ, E), F32), S((RQ, E), F32), S((R, D), F32)],
            in_specs=[VM] * 7,
            out_specs=[ANY] * 4 + [VM],
            scratch_shapes=[V((NB, E, CW), F32), V((NB, 2, RQ, E), F32), V((2, RQ, E), F32), DMA((NB,)), DMA((NB,)), DMA((2,))],
            compiler_params=pltpu.CompilerParams(vmem_limit_bytes=24 * 2**20),
            cost_estimate=pl.CostEstimate(flops=4 * 10**10, bytes_accessed=8 * 10**7, transcendentals=0),
            name="grads",
        )(xt, dyg, ot, dq, dkv, wkv, dxk)
        dx = (dxo + far).astype(BF)
        dw_query = jnp.transpose(dwq.reshape(HL, D, E), (1, 0, 2))
        return dx, dw_query, dwk, dwv, dwo.reshape(HL, E, D)

    return jax.shard_map(step, mesh=mesh, in_specs=(tok, tok, P(None, "model", None), P(None, None), P(None, None), P("model", None, None)),
                         out_specs=(tok, P("data", "model", None), tok, tok, P(("data", "model"), None, None)), check_vma=False)
```

profile of v0, /device:TPU:0, one launch (start us, length us, event | category | flops | bytes accessed | tf_op | source)
XLA Modules:
  0.0 55.1 jit_solution(5107088516092327835)
XLA Ops:
  0.6 28.4 %attend.1 = (bf16[6144,64]{1,0:T(8,128)(2,1)S(1)}, bf16[64,6144]{1,0:T(8,128)(2,1)S(1)}, bf16[1536,64]{1,0:T(8,128)(2,1)S(1)}, bf16[64,1536]{1,0:T(8,128)(2,1)S(...) custom-call(bf16[16,6144]{1,0:T(8,128)(2,1)} %x_ref.1, ...), custom_call_target="tpu_custom_call" | custom-call | flops 10000000000 | bytes 40000000 | tf_op jit(solution)/shard_map/attend/pallas_call | solution.py:290
  29.0 1.0 %collective-permute-start = (f32[16,6144]{1,0:T(8,128)}, f32[16,6144]{1,0:T(8,128)S(1)}, u32[]{:S(2)}, u32[]{:S(2)}) collective-permute-start(f32[16,6144]{1,0:T(8,128)} %get-tuple-element.26), channel_id=1, source_target_pairs={{0,2},{2,0},{1,3},{3,1},{4,6},{6,4},{5,7},{7,5}} | collective-permute-start | bytes 1179656 | tf_op jit(solution)/shard_map/ppermute | solution.py:306
  30.0 24.4 %grads.1 = (f32[6,2,6144,128]{3,2,1,0:T(8,128)}, f32[1536,6144]{1,0:T(8,128)}, f32[1536,128]{1,0:T(8,128)}, f32[1536,128]{1,0:T(8,128)}, f32[16,6144]{1,0:T(8,128)S(1)}) custom-call(bf16[6144,64]{1,0:T(8,128)(2,1)S(1)} %get-tuple-element.18.xt_ref, bf16[64,6144]{1,0:T(8,128)(2,1)S(1)} %get-tuple-element.19.dyg_ref, ...), custom_call_target="tpu_custom_call" | custom-call | flops 40000000000 | bytes 80000000 | tf_op jit(solution)/shard_map/grads/pallas_call | solution.py:307
  54.4 0.0 collective-permute-done
  54.4 0.7 %add_convert_fusion = bf16[16,6144]{1,0:T(8,128)(2,1)} fusion(f32[16,6144]{1,0:T(8,128)S(1)} %get-tuple-element.25, f32[16,6144]{1,0:T(8,128)S(1)} %collective-permute-done), kind=kLoop, calls=%fused_computation | loop fusion | flops 196608 | bytes 983040 | tf_op jit(solution)/shard_map/convert_element_type | solution.py:317
Async XLA Ops:
  29.0 25.4 %collective-permute-start = (f32[16,6144]{1,0:T(8,128)}, f32[16,6144]{1,0:T(8,128)S(1)}, u32[]{:S(2)}, u32[]{:S(2)}) collective-permute-start(f32[16,6144]{1,0:T(8,128)} %get-tuple-element.26), channel_id=1, source_target_pairs={{0,2},{2,0},{1,3},{3,1},{4,6},{6,4},{5,7},{7,5}} | collective-permute-start | bytes 1179656 | tf_op jit(solution)/shard_map/ppermute | solution.py:306
where the time goes:
time: 55.2 us; the launch traced here: 55.1 us
  Pallas kernels  52.7 us (95%)
  starting transfers between devices  0.98 us (2%)
  other arithmetic  0.71 us (1%)
  between operations  0.66 us (1%)
    pallas_call x1, Pallas kernels, step(): pl.pallas_call(attend_kernel, out_shape=[V((D, T), BF), V((T, D), BF), V(...  28.4 us
    pallas_call x1, Pallas kernels, step(): pl.pallas_call(grads_kernel, out_shape=[S((NP, 2, D, E), F32), S((HL * E,...  24.4 us
  transfers between devices with their start and end apart: 1, of which 0 were waited for; matrix products, arithmetic and copies ran while one was open for 0% of the time, Pallas kernels for 44%

commit v1 on v0

--- a/solution.py
+++ b/solution.py
@@ -17,13 +17,17 @@
 
 T, D, HL, E, R = 64, 6144, 12, 128, 16
 NP = HL // 2
-NC = 4
 LEAD = 1
-DC = D // NC
-NX = 8
-XC = D // NX
+SIZES = ((1536, 1536, 1536, 1536), (2048, 2048, 1536, 512))
+STARTS = tuple(tuple(sum(sz[:c]) for c in range(len(sz))) for sz in SIZES)
+NY, NQ = len(SIZES[0]), len(SIZES[1])
+NC = max(NY, NQ)
 N1 = 512
 N2 = 256
+XB = N1 + N2
+XS = (3, 3, 2)
+NX = len(XS)
+X0 = tuple(sum(XS[:c]) for c in range(NX))
 
 
 def attend_kernel(x_ref, dy_ref, wq_ref, wk_ref, wv_ref, wo_ref,
@@ -40,17 +44,17 @@
     far = pl.ds(pl.multiple_of(counter * R, R), R)
     bufs = (dyg_ref, xg)
 
-    def cols(c):
-        return pl.ds(c * DC, DC)
+    def cols(a, c):
+        return pl.ds(STARTS[a][c], SIZES[a][c])
 
     loads = [pltpu.make_async_copy(s, g.at[own], lsem.at[a]) for a, (s, g) in enumerate(((dy_ref, dyg_ref), (x_ref, xg)))]
     for cp in loads:
         cp.start()
     wkv_cp = [pltpu.make_async_copy(s, wkv.at[:, pl.ds(j * E, E)], wsem.at[j]) for j, s in enumerate((wk_ref, wv_ref))]
-    wq_cp = [[pltpu.make_async_copy(wq_ref.at[:, j, cols(c), :], wq.at[:, cols(c), pl.ds(j * E, E)], wsem.at[2 + 2 * c + j])
-              for j in range(2)] for c in range(NC)]
-    wo_cp = [pltpu.make_async_copy(wo_ref.at[:, cols(c)], wo.at[:, cols(c)], wsem.at[2 + 2 * NC + c]) for c in range(NC)]
-    for cp in wo_cp[:NC // 2]:
+    wq_cp = [[pltpu.make_async_copy(wq_ref.at[:, j, cols(1, c), :], wq.at[:, cols(1, c), pl.ds(j * E, E)], wsem.at[2 + 2 * c + j])
+              for j in range(2)] for c in range(NQ)]
+    wo_cp = [pltpu.make_async_copy(wo_ref.at[:, cols(0, c)], wo.at[:, cols(0, c)], wsem.at[2 + 2 * NQ + c]) for c in range(NY)]
+    for cp in wo_cp[:NY // 2]:
         cp.start(priority=1)
 
     barrier = pltpu.get_barrier_semaphore()
@@ -62,41 +66,41 @@
     for a in range(2):
         g = bufs[a]
         loads[a].wait()
-        link.append([pltpu.make_async_remote_copy(g.at[own, cols(c)], g.at[own, cols(c)], link_s.at[a, c], link_r.at[a, c],
-                                                  device_id={"model": counter}, device_id_type=MESH) for c in range(NC)])
+        link.append([pltpu.make_async_remote_copy(g.at[own, cols(a, c)], g.at[own, cols(a, c)], link_s.at[a, c], link_r.at[a, c],
+                                                  device_id={"model": counter}, device_id_type=MESH) for c in range(len(SIZES[a]))])
         pair.append(pltpu.make_async_remote_copy(g.at[own], g.at[own], pair_s.at[a], pair_r.at[a],
                                                  device_id={"model": partner}, device_id_type=MESH))
-        fwd.append([pltpu.make_async_remote_copy(g.at[far, cols(c)], g.at[far, cols(c)], fwd_s.at[a, c], fwd_r.at[a, c],
-                                                 device_id={"model": partner}, device_id_type=MESH) for c in range(NC)])
+        fwd.append([pltpu.make_async_remote_copy(g.at[far, cols(a, c)], g.at[far, cols(a, c)], fwd_s.at[a, c], fwd_r.at[a, c],
+                                                 device_id={"model": partner}, device_id_type=MESH) for c in range(len(SIZES[a]))])
         for cp in link[a]:
             cp.start()
         pair[a].start()
 
-    for cp in wo_cp[NC // 2:] + wkv_cp:
+    for cp in wo_cp[NY // 2:] + wkv_cp:
         cp.start(priority=1)
 
     def relay(i):
-        a, c = divmod(i, NC)
-        if a < 2:
+        a, c = (0, i) if i < NY else (1, i - NY)
+        if c < len(SIZES[a]):
             link[a][c].wait_recv()
             fwd[a][c].start()
 
     for i in range(LEAD):
         relay(i)
     pair[0].wait_recv()
-    for c in range(NC):
+    for c in range(NY):
         relay(c + LEAD)
         fwd[0][c].wait_recv()
         wo_cp[c].wait()
-        for cp in wq_cp[c]:
+        for cp in wq_cp[c] + (sum(wq_cp[NY:], []) if c == NY - 1 else []):
             cp.start(priority=1)
-        dyc = dyg_ref[:, cols(c)]
+        dyc = dyg_ref[:, cols(0, c)]
         dyct = dyc.T
         for p in range(2):
             base = p * (N1 + N2)
             by_rows, by_cols = None, None
-            for k in range(DC // 256):
-                ks = pl.ds(c * DC + k * 256, 256)
+            for k in range(SIZES[0][c] // 256):
+                ks = pl.ds(STARTS[0][c] + k * 256, 256)
                 t1 = lax.dot_general(dyc[:, k * 256:(k + 1) * 256], wo[pl.ds(base, N1), ks], NT, preferred_element_type=F32)
                 t2 = jnp.dot(wo[pl.ds(base + N1, N2), ks], dyct[k * 256:(k + 1) * 256, :], preferred_element_type=F32)
                 by_rows = t1 if by_rows is None else by_rows + t1
@@ -117,24 +121,24 @@
     pair[1].wait_recv()
     for cp in wkv_cp:
         cp.wait()
-    for c in range(NC):
-        relay(NC + c + LEAD)
+    for c in range(NQ):
+        relay(NY + c + LEAD)
         fwd[1][c].wait_recv()
         for cp in wq_cp[c]:
             cp.wait()
-        xc = xg[:, cols(c)]
+        xc = xg[:, cols(1, c)]
         for p in range(NP):
-            part_q = jnp.dot(xc, wq[p, cols(c), :], preferred_element_type=F32)
+            part_q = jnp.dot(xc, wq[p, cols(1, c), :], preferred_element_type=F32)
             if c == 0:
                 qacc[p] = part_q
             else:
                 qacc[p] += part_q
-        part_kv = jnp.dot(xc, wkv[cols(c), :], preferred_element_type=F32)
+        part_kv = jnp.dot(xc, wkv[cols(1, c), :], preferred_element_type=F32)
         if c == 0:
             kvacc[...] = part_kv
         else:
             kvacc[...] += part_kv
-        xt_ref[cols(c), :] = xc.T
+        xt_ref[cols(1, c), :] = xc.T
     kv = kvacc[...].astype(BF)
     keys, vals = kv[:, :E], kv[:, E:]
     for p in range(NP):
@@ -163,17 +167,20 @@
         for r in range(4):
             slot = (r // 2 + chip) % 2 * 2 + (r % 2 + core) % 2
             dqp[slot, :, pl.ds(h * E, E)] = dqh[r * R:(r + 1) * R, :]
-    ex = [pltpu.make_async_remote_copy(part.at[2 * i], part.at[2 * i + 1], ex_s.at[i], ex_r.at[i], device_id={"model": peer}, device_id_type=MESH)
-          for i, peer in enumerate((partner, counter))]
-    ex[0].start()
+    ex = [pltpu.make_async_remote_copy(part.at[0], part.at[i + 1], ex_s.at[i], ex_r.at[i], device_id={"model": peer}, device_id_type=MESH)
+          for i, peer in enumerate((partner, counter, diag))]
+    for cp in ex:
+        cp.start()
     lhs = dqp[...].reshape(T, HL * E)
-    red = [pltpu.make_async_remote_copy(send.at[:, :, pl.ds(c * XC, XC)], got.at[:, :, pl.ds(c * XC, XC)], red_s.at[c], red_r.at[c],
+    def xcols(c):
+        return pl.ds(X0[c] * XB, XS[c] * XB)
+
+    red = [pltpu.make_async_remote_copy(send.at[:, :, xcols(c)], got.at[:, :, xcols(c)], red_s.at[c], red_r.at[c],
                                         device_id={"model": partner}, device_id_type=MESH) for c in range(NX)]
 
     lhst = lhs.T
 
-    def dx_chunk(c):
-        base = c * XC
+    def dx_block(base):
         by_rows, by_cols = None, None
         for p in range(NP):
             ps = slice(p * 2 * E, (p + 1) * 2 * E)
@@ -188,35 +195,29 @@
             dst[k // 2, :, pl.ds(base + N1, N2)] = by_cols[r, :]
 
     def dx_sum(c):
-        rows = pl.ds(c * XC, XC)
+        rows = xcols(c)
         red[c].wait_recv()
         dxk_ref[:, rows] = keep[0, :, rows] + got[0, :, rows]
         dxs_ref[:, rows] = keep[1, :, rows] + got[1, :, rows]
 
     for c in range(NX):
-        dx_chunk(c)
-        if c == 0:
-            for h in range(HL):
-                ot_ref[pl.ds(h * E, E), :] = o_s[pl.ds(h * T, T), :].T
-        if c == 1:
-            ex[0].wait_recv()
-            part[2] = part[0] + part[1]
-        if c == 2:
-            ex[1].start()
+        for i in range(XS[c]):
+            dx_block((X0[c] + i) * XB)
         if c >= 1:
             red[c - 1].start()
-    for c in range(NX - 2):
+    for h in range(HL):
+        ot_ref[pl.ds(h * E, E), :] = o_s[pl.ds(h * T, T), :].T
+    red[NX - 1].start()
+    for c in range(NX - 1):
         dx_sum(c)
-    red[NX - 1].start()
-    dx_sum(NX - 2)
-    ex[1].wait_recv()
-    dkv_ref[...] = (part[2] + part[3]).astype(BF)
+    for cp in ex:
+        cp.wait_recv()
+    dkv_ref[...] = ((part[0] + part[1]) + (part[2] + part[3])).astype(BF)
     dx_sum(NX - 1)
     for a in range(2):
         pair[a].wait_send()
-        for c in range(NC):
-            link[a][c].wait_send()
-            fwd[a][c].wait_send()
+        for cp in link[a] + fwd[a]:
+            cp.wait_send()
     for cp in ex + red:
         cp.wait_send()
 
@@ -289,15 +290,15 @@
         V = pltpu.VMEM
         xt, dyg, ot, dq, dkv, wkv, dxk, dxs = pl.pallas_call(
             attend_kernel,
-            out_shape=[V((D, T), BF), V((T, D), BF), V((HL * E, T), BF), V((T, HL * E), BF), V((T, 2 * E), BF), V((D, 2 * E), BF), V((R, D), F32), S((R, D), F32)],
+            out_shape=[V((D, T), BF), V((T, D), BF), V((HL * E, T), BF), V((T, HL * E), BF), V((T, 2 * E), BF), V((D, 2 * E), BF), V((R, D), F32), V((R, D), F32)],
             in_specs=[ANY] * 6,
             out_specs=[VM] * 8,
             scratch_shapes=[
                 V((T, D), BF), V((NP, D, 2 * E), BF), V((HL * E, D), BF), V((NP, T, 2 * E), F32), V((T, 2 * E), F32),
                 V((2, T, N1), F32), V((2, N2, T), F32), V((HL * T, E), BF), V((HL * T, E), BF), V((HL * T, E), BF),
                 V((4, R, HL * E), BF), V((4, T, 2 * E), F32), V((2, R, D), F32), V((2, R, D), F32), V((2, R, D), F32),
-                DMA((2,)), DMA((2 + 3 * NC,)), DMA((2, NC)), DMA((2, NC)), DMA((2,)), DMA((2,)), DMA((2, NC)), DMA((2, NC)),
-                DMA((2,)), DMA((2,)), DMA((NX,)), DMA((NX,)),
+                DMA((2,)), DMA((2 + 2 * NQ + NY,)), DMA((2, NC)), DMA((2, NC)), DMA((2,)), DMA((2,)), DMA((2, NC)), DMA((2, NC)),
+                DMA((3,)), DMA((3,)), DMA((NX,)), DMA((NX,)),
             ],
             compiler_params=pltpu.CompilerParams(collective_id=0, has_side_effects=True, vmem_limit_bytes=50 * 2**20),
             cost_estimate=pl.CostEstimate(flops=10**10, bytes_accessed=4 * 10**7, transcendentals=0),

time: 55.2 us -> 52.2 us (0.946)
  Pallas kernels: 52.7 us -> 49.8 us
    pallas_call x1, Pallas kernels: 28.4 us -> 25.4 us  [step(): pl.pallas_call(attend_kernel, out_shape=[V((D, T), BF), V((T, D), BF), V(...]
  transfers between devices with their start and end apart: 1 -> 1, of which waited for: 0 -> 0; matrix products, arithmetic and copies ran while one was open for 0% -> 0% of each run, Pallas kernels for 44% -> 47%
where the time goes in v1:
time: 52.2 us; the launch traced here: 52.1 us
  Pallas kernels  49.8 us (95%)
  starting transfers between devices  0.99 us (2%)
  other arithmetic  0.71 us (1%)
  between operations  0.66 us (1%)
    pallas_call x1, Pallas kernels, step(): pl.pallas_call(attend_kernel, out_shape=[V((D, T), BF), V((T, D), BF), V(...  25.4 us
    pallas_call x1, Pallas kernels, step(): pl.pallas_call(grads_kernel, out_shape=[S((NP, 2, D, E), F32), S((HL * E,...  24.4 us
  transfers between devices with their start and end apart: 1, of which 0 were waited for; matrix products, arithmetic and copies ran while one was open for 0% of the time, Pallas kernels for 47%

profile of v1, /device:TPU:0, one launch (start us, length us, event | category | flops | bytes accessed | tf_op | source)
XLA Modules:
  0.0 52.1 jit_solution(16542650815817522263)
XLA Ops:
  0.6 25.4 %attend.1 = (bf16[6144,64]{1,0:T(8,128)(2,1)S(1)}, bf16[64,6144]{1,0:T(8,128)(2,1)S(1)}, bf16[1536,64]{1,0:T(8,128)(2,1)S(1)}, bf16[64,1536]{1,0:T(8,128)(2,1)S(...) custom-call(bf16[16,6144]{1,0:T(8,128)(2,1)} %x_ref.1, ...), custom_call_target="tpu_custom_call" | custom-call | flops 10000000000 | bytes 40000000 | tf_op jit(solution)/shard_map/attend/pallas_call | solution.py:291
  26.0 1.0 %collective-permute-start = (f32[16,6144]{1,0:T(8,128)S(1)}, f32[16,6144]{1,0:T(8,128)S(1)}, u32[]{:S(2)}, u32[]{:S(2)}) collective-permute-start(f32[16,6144]{1,0:T(8,128)S(1)} %get-tuple-element.26), channel_id=1, source_target_pairs={{0,2},{2,0},{1,3},{3,1},{4,6},{6,4},{5,7},{7,5}} | collective-permute-start | bytes 1179656 | tf_op jit(solution)/shard_map/ppermute | solution.py:307
  27.0 24.4 %grads.1 = (f32[6,2,6144,128]{3,2,1,0:T(8,128)}, f32[1536,6144]{1,0:T(8,128)}, f32[1536,128]{1,0:T(8,128)}, f32[1536,128]{1,0:T(8,128)}, f32[16,6144]{1,0:T(8,128)S(1)}) custom-call(bf16[6144,64]{1,0:T(8,128)(2,1)S(1)} %get-tuple-element.18.xt_ref, bf16[64,6144]{1,0:T(8,128)(2,1)S(1)} %get-tuple-element.19.dyg_ref, ...), custom_call_target="tpu_custom_call" | custom-call | flops 40000000000 | bytes 80000000 | tf_op jit(solution)/shard_map/grads/pallas_call | solution.py:308
  51.4 0.0 collective-permute-done
  51.4 0.7 %add_convert_fusion = bf16[16,6144]{1,0:T(8,128)(2,1)} fusion(f32[16,6144]{1,0:T(8,128)S(1)} %get-tuple-element.25, f32[16,6144]{1,0:T(8,128)S(1)} %collective-permute-done), kind=kLoop, calls=%fused_computation | loop fusion | flops 196608 | bytes 983040 | tf_op jit(solution)/shard_map/convert_element_type | solution.py:318
Async XLA Ops:
  26.0 25.4 %collective-permute-start = (f32[16,6144]{1,0:T(8,128)S(1)}, f32[16,6144]{1,0:T(8,128)S(1)}, u32[]{:S(2)}, u32[]{:S(2)}) collective-permute-start(f32[16,6144]{1,0:T(8,128)S(1)} %get-tuple-element.26), channel_id=1, source_target_pairs={{0,2},{2,0},{1,3},{3,1},{4,6},{6,4},{5,7},{7,5}} | collective-permute-start | bytes 1179656 | tf_op jit(solution)/shard_map/ppermute | solution.py:307

commit v2 on v1

--- a/solution.py
+++ b/solution.py
@@ -178,14 +178,13 @@
     red = [pltpu.make_async_remote_copy(send.at[:, :, xcols(c)], got.at[:, :, xcols(c)], red_s.at[c], red_r.at[c],
                                         device_id={"model": partner}, device_id_type=MESH) for c in range(NX)]
 
-    lhst = lhs.T
 
     def dx_block(base):
         by_rows, by_cols = None, None
         for p in range(NP):
             ps = slice(p * 2 * E, (p + 1) * 2 * E)
             t1 = lax.dot_general(lhs[:, ps], wq[p, pl.ds(base, N1), :], NT, preferred_element_type=F32)
-            t2 = jnp.dot(wq[p, pl.ds(base + N1, N2), :], lhst[ps, :], preferred_element_type=F32)
+            t2 = lax.dot_general(wq[p, pl.ds(base + N1, N2), :], lhs[:, ps], NT, preferred_element_type=F32)
             by_rows = t1 if by_rows is None else by_rows + t1
             by_cols = t2 if by_cols is None else by_cols + t2
         by_cols = by_cols.T

time: 52.2 us -> 51.8 us (level)
  no operation moved by 1% of the time
where the time goes in v2:
time: 51.8 us; the launch traced here: 51.7 us
  Pallas kernels  49.3 us (95%)
  starting transfers between devices  0.99 us (2%)
  other arithmetic  0.71 us (1%)
  between operations  0.66 us (1%)
    pallas_call x1, Pallas kernels, step(): pl.pallas_call(attend_kernel, out_shape=[V((D, T), BF), V((T, D), BF), V(...  24.9 us
    pallas_call x1, Pallas kernels, step(): pl.pallas_call(grads_kernel, out_shape=[S((NP, 2, D, E), F32), S((HL * E,...  24.4 us
  transfers between devices with their start and end apart: 1, of which 0 were waited for; matrix products, arithmetic and copies ran while one was open for 0% of the time, Pallas kernels for 47%

profile of v2, /device:TPU:0, one launch (start us, length us, event | category | flops | bytes accessed | tf_op | source)
XLA Modules:
  0.0 51.7 jit_solution(1887260123351933275)
XLA Ops:
  0.6 24.9 %attend.1 = (bf16[6144,64]{1,0:T(8,128)(2,1)S(1)}, bf16[64,6144]{1,0:T(8,128)(2,1)S(1)}, bf16[1536,64]{1,0:T(8,128)(2,1)S(1)}, bf16[64,1536]{1,0:T(8,128)(2,1)S(...) custom-call(bf16[16,6144]{1,0:T(8,128)(2,1)} %x_ref.1, ...), custom_call_target="tpu_custom_call" | custom-call | flops 10000000000 | bytes 40000000 | tf_op jit(solution)/shard_map/attend/pallas_call | solution.py:290
  25.6 1.0 %collective-permute-start = (f32[16,6144]{1,0:T(8,128)S(1)}, f32[16,6144]{1,0:T(8,128)S(1)}, u32[]{:S(2)}, u32[]{:S(2)}) collective-permute-start(f32[16,6144]{1,0:T(8,128)S(1)} %get-tuple-element.26), channel_id=1, source_target_pairs={{0,2},{2,0},{1,3},{3,1},{4,6},{6,4},{5,7},{7,5}} | collective-permute-start | bytes 1179656 | tf_op jit(solution)/shard_map/ppermute | solution.py:306
  26.6 24.4 %grads.1 = (f32[6,2,6144,128]{3,2,1,0:T(8,128)}, f32[1536,6144]{1,0:T(8,128)}, f32[1536,128]{1,0:T(8,128)}, f32[1536,128]{1,0:T(8,128)}, f32[16,6144]{1,0:T(8,128)S(1)}) custom-call(bf16[6144,64]{1,0:T(8,128)(2,1)S(1)} %get-tuple-element.18.xt_ref, bf16[64,6144]{1,0:T(8,128)(2,1)S(1)} %get-tuple-element.19.dyg_ref, ...), custom_call_target="tpu_custom_call" | custom-call | flops 40000000000 | bytes 80000000 | tf_op jit(solution)/shard_map/grads/pallas_call | solution.py:307
  50.9 0.0 collective-permute-done
  51.0 0.7 %add_convert_fusion = bf16[16,6144]{1,0:T(8,128)(2,1)} fusion(f32[16,6144]{1,0:T(8,128)S(1)} %get-tuple-element.25, f32[16,6144]{1,0:T(8,128)S(1)} %collective-permute-done), kind=kLoop, calls=%fused_computation | loop fusion | flops 196608 | bytes 983040 | tf_op jit(solution)/shard_map/convert_element_type | solution.py:317
Async XLA Ops:
  25.6 25.4 %collective-permute-start = (f32[16,6144]{1,0:T(8,128)S(1)}, f32[16,6144]{1,0:T(8,128)S(1)}, u32[]{:S(2)}, u32[]{:S(2)}) collective-permute-start(f32[16,6144]{1,0:T(8,128)S(1)} %get-tuple-element.26), channel_id=1, source_target_pairs={{0,2},{2,0},{1,3},{3,1},{4,6},{6,4},{5,7},{7,5}} | collective-permute-start | bytes 1179656 | tf_op jit(solution)/shard_map/ppermute | solution.py:306

commit v3 on v2

--- a/solution.py
+++ b/solution.py
@@ -161,16 +161,16 @@
     part[0, :, E:] = lax.dot_general(pb, d_attn, TN, preferred_element_type=F32)
     part[0, :, :E] = lax.dot_general(g, q_s[...], TN, preferred_element_type=F32)
     d_query = jnp.dot(g, keys, preferred_element_type=F32).astype(BF)
+    ex = [pltpu.make_async_remote_copy(part.at[0], part.at[i + 1], ex_s.at[i], ex_r.at[i], device_id={"model": peer}, device_id_type=MESH)
+          for i, peer in enumerate((partner, counter, diag))]
+    for cp in ex:
+        cp.start()
     for h in range(HL):
         dqh = d_query[h * T:(h + 1) * T, :]
         dq_ref[:, pl.ds(h * E, E)] = dqh
         for r in range(4):
             slot = (r // 2 + chip) % 2 * 2 + (r % 2 + core) % 2
             dqp[slot, :, pl.ds(h * E, E)] = dqh[r * R:(r + 1) * R, :]
-    ex = [pltpu.make_async_remote_copy(part.at[0], part.at[i + 1], ex_s.at[i], ex_r.at[i], device_id={"model": peer}, device_id_type=MESH)
-          for i, peer in enumerate((partner, counter, diag))]
-    for cp in ex:
-        cp.start()
     lhs = dqp[...].reshape(T, HL * E)
     def xcols(c):
         return pl.ds(X0[c] * XB, XS[c] * XB)

time: 51.8 us -> 51.6 us (level)
  no operation moved by 1% of the time
where the time goes in v3:
time: 51.6 us
  Pallas kernels  49.2 us (95%)
  starting transfers between devices  0.99 us (2%)
  other arithmetic  0.71 us (1%)
  between operations  0.66 us (1%)
    pallas_call x1, Pallas kernels, step(): pl.pallas_call(attend_kernel, out_shape=[V((D, T), BF), V((T, D), BF), V(...  24.8 us
    pallas_call x1, Pallas kernels, step(): pl.pallas_call(grads_kernel, out_shape=[S((NP, 2, D, E), F32), S((HL * E,...  24.4 us
  transfers between devices with their start and end apart: 1, of which 0 were waited for; matrix products, arithmetic and copies ran while one was open for 0% of the time, Pallas kernels for 47%

profile of v3, /device:TPU:0, one launch (start us, length us, event | category | flops | bytes accessed | tf_op | source)
XLA Modules:
  0.0 51.6 jit_solution(10842957030064351949)
XLA Ops:
  0.6 24.8 %attend.1 = (bf16[6144,64]{1,0:T(8,128)(2,1)S(1)}, bf16[64,6144]{1,0:T(8,128)(2,1)S(1)}, bf16[1536,64]{1,0:T(8,128)(2,1)S(1)}, bf16[64,1536]{1,0:T(8,128)(2,1)S(...) custom-call(bf16[16,6144]{1,0:T(8,128)(2,1)} %x_ref.1, ...), custom_call_target="tpu_custom_call" | custom-call | flops 10000000000 | bytes 40000000 | tf_op jit(solution)/shard_map/attend/pallas_call | solution.py:290
  25.4 1.0 %collective-permute-start = (f32[16,6144]{1,0:T(8,128)S(1)}, f32[16,6144]{1,0:T(8,128)S(1)}, u32[]{:S(2)}, u32[]{:S(2)}) collective-permute-start(f32[16,6144]{1,0:T(8,128)S(1)} %get-tuple-element.26), channel_id=1, source_target_pairs={{0,2},{2,0},{1,3},{3,1},{4,6},{6,4},{5,7},{7,5}} | collective-permute-start | bytes 1179656 | tf_op jit(solution)/shard_map/ppermute | solution.py:306
  26.4 24.4 %grads.1 = (f32[6,2,6144,128]{3,2,1,0:T(8,128)}, f32[1536,6144]{1,0:T(8,128)}, f32[1536,128]{1,0:T(8,128)}, f32[1536,128]{1,0:T(8,128)}, f32[16,6144]{1,0:T(8,128)S(1)}) custom-call(bf16[6144,64]{1,0:T(8,128)(2,1)S(1)} %get-tuple-element.18.xt_ref, bf16[64,6144]{1,0:T(8,128)(2,1)S(1)} %get-tuple-element.19.dyg_ref, ...), custom_call_target="tpu_custom_call" | custom-call | flops 40000000000 | bytes 80000000 | tf_op jit(solution)/shard_map/grads/pallas_call | solution.py:307
  50.8 0.0 collective-permute-done
  50.8 0.7 %add_convert_fusion = bf16[16,6144]{1,0:T(8,128)(2,1)} fusion(f32[16,6144]{1,0:T(8,128)S(1)} %get-tuple-element.25, f32[16,6144]{1,0:T(8,128)S(1)} %collective-permute-done), kind=kLoop, calls=%fused_computation | loop fusion | flops 196608 | bytes 983040 | tf_op jit(solution)/shard_map/convert_element_type | solution.py:317
Async XLA Ops:
  25.4 25.4 %collective-permute-start = (f32[16,6144]{1,0:T(8,128)S(1)}, f32[16,6144]{1,0:T(8,128)S(1)}, u32[]{:S(2)}, u32[]{:S(2)}) collective-permute-start(f32[16,6144]{1,0:T(8,128)S(1)} %get-tuple-element.26), channel_id=1, source_target_pairs={{0,2},{2,0},{1,3},{3,1},{4,6},{6,4},{5,7},{7,5}} | collective-permute-start | bytes 1179656 | tf_op jit(solution)/shard_map/ppermute | solution.py:306
